TPU v7x, 256 devices: a whole 4x4x8 slice. The times are simulated.
256 devices in a mesh: row: 8 (over y, x_lo), col: 32 (over z, x_hi, core).
Axes of the slice: x: 4 (x_hi: 2, x_lo: 2; x = x_hi * 2 + x_lo), y: 4, z: 8, core: 2. Of those that a mesh axis runs over, the one named last changes fastest.
Arguments:
- pair_rep: bfloat16 [1024, 1024, 128], P('row', 'col'), may hold values from -6 to 6
- proj_weight: bfloat16 [2, 4, 128, 128], replicated, may hold values from -0.5 to 0.5
- gate_weight: bfloat16 [2, 128, 128], replicated, may hold values from -0.5 to 0.5
- out_weight: bfloat16 [2, 128, 128], replicated, may hold values from -0.5 to 0.5
- in_gain: float32 [2, 128], replicated, may hold values from 0.1 to 1.9
- out_gain: float32 [2, 128], replicated, may hold values from 0.1 to 1.9
Outputs:
- updated_pair: bfloat16 [1024, 1024, 128], P('row', 'col')
All inputs are finite; a program needn't handle non-finite values.
Results may differ from a plain program's by a relative error of at most 0.011.
Values may be sent and summed in bfloat16 or wider, within the bound.
No kernel may reach another device: no remote copies, remote signals or barrier semaphores. Data moves between devices by JAX's collectives and lax.ppermute only.
A program may use at most 64 MiB of HBM per device.

v0:
```python
import jax
import jax.numpy as jnp
from jax import lax
from jax.sharding import Mesh
from jax.sharding import PartitionSpec as P

ROW = ("row_0", "row_1")
epsilon = 1e-05


def sum_by_axis(terms, axes):
    subtotal = terms.astype(jnp.bfloat16)
    for axis in axes:
        subtotal = lax.psum_scatter(subtotal, axis, scatter_dimension=0, tiled=True)
    return subtotal.astype(jnp.float32)


def layer_norm(values, gain_row, reduce_axis):
    center = values - jnp.mean(values, axis=reduce_axis, keepdims=True)
    spread = jnp.mean(center * center, axis=reduce_axis, keepdims=True)
    return center * lax.rsqrt(spread + epsilon) * gain_row


def local(pair_rep, proj_weight, gate_weight, out_weight, in_gain, out_gain):
    current = pair_rep
    for update_index in range(2):
        widened = current.astype(jnp.float32)
        normed = layer_norm(widened, in_gain[update_index], 2).astype(jnp.bfloat16)
        projected = jnp.einsum(
            "ijc,pch->phij", normed, proj_weight[update_index], preferred_element_type=jnp.float32
        )
        left_hand = (jax.nn.sigmoid(projected[0]) * projected[1]).astype(jnp.bfloat16)
        right_hand = (jax.nn.sigmoid(projected[2]) * projected[3]).astype(jnp.bfloat16)
        gating = jax.nn.sigmoid(
            jnp.dot(normed, gate_weight[update_index], preferred_element_type=jnp.float32)
        )
        left_rows, right_rows = (
            lax.all_to_all(left_hand, "col", split_axis=0, concat_axis=2, tiled=True),
            lax.all_to_all(right_hand, "col", split_axis=0, concat_axis=2, tiled=True),
        )
        if update_index == 0:
            triangle = jnp.einsum(
                "gik,gjk->igj",
                left_rows,
                lax.all_gather(right_rows, ROW, axis=1, tiled=True),
                preferred_element_type=jnp.float32,
            )
        else:
            triangle = sum_by_axis(
                jnp.einsum(
                    "gki,gkj->igj", left_rows, right_rows, preferred_element_type=jnp.float32
                ),
                ROW,
            )
        returned = lax.all_to_all(
            triangle.astype(jnp.bfloat16), "col", split_axis=2, concat_axis=1, tiled=True
        )
        mixed_rows = layer_norm(
            returned.astype(jnp.float32), out_gain[update_index][None, :, None], 1
        ).astype(jnp.bfloat16)
        update = jnp.einsum(
            "ihj,hc->ijc", mixed_rows, out_weight[update_index], preferred_element_type=jnp.float32
        )
        current = (widened + gating * update).astype(jnp.bfloat16)
    return current


def solution(mesh):
    finer = Mesh(mesh.devices.reshape(4, 2, mesh.shape["col"]), ("row_0", "row_1", "col"))
    placed = (P(ROW, "col", None), P(), P(), P(), P(), P())
    return jax.shard_map(
        local, mesh=finer, in_specs=placed, out_specs=P(ROW, "col", None), check_vma=False
    )
```

profile of v0, /device:TPU:4, one launch (start us, length us, event | category | flops | bytes accessed | tf_op | source)
XLA Modules:
  0.0 535.5 jit_solution(13058157798516220307)
XLA Ops:
  6.5 2.0 copy.75
  8.5 0.2 convert_reduce_fusion.1
  8.7 0.3 fusion.7
  9.1 1.4 convolution_bitcast_fusion.1
  10.5 1.1 fusion.49
  11.6 1.7 copy.79
  13.3 40.5 %all_to_all.90 = bf16[128,128,32]{1,2,0:T(8,128)(2,1)S(1)} all-to-all(bf16[128,128,32]{1,2,0:T(8,128)(2,1)} %copy.79), channel_id=1, replica_groups=mesh['row_0'=4,'row_1'=2,'col'=32] {'col'}, dimensions={0} | all-to-all | bytes 2097152 | tf_op jit(solution)/shard_map/all_to_all | solution.py:39
  53.9 1.3 copy.81
  55.2 1.0 copy.82
  56.2 33.7 %all_to_all.91 = bf16[128,128,32]{1,2,0:T(8,128)(2,1)S(1)} all-to-all(bf16[128,128,32]{1,2,0:T(8,128)(2,1)S(1)} %copy.82), channel_id=1, replica_groups=mesh['row_0'=4,'row_1'=2,'col'=32] {'col'}, dimensions={0} | all-to-all | bytes 2097152 | tf_op jit(solution)/shard_map/all_to_all | solution.py:38
  90.0 142.3 %all-gather.2.cloned.1.call-done = bf16[4,1024,1024]{2,1,0:T(8,128)(2,1)} async-done(((bf16[4,128,1024]{2,1,0:T(8,128)(2,1)}), bf16[4,1024,1024]{2,1,0:T(8,128)(2,1)}) %all-gather.2.cloned.1.call-update) | async-done | bytes 8388624 | tf_op jit(solution)/shard_map/all_gather | solution.py:45
  232.4 5.7 %fusion.42 = bf16[128,4,1024]{0,2,1:T(8,128)(2,1)S(1)} fusion(bf16[4,1024,1024]{2,1,0:T(8,128)(2,1)} %all-gather.2.cloned.1.call-done, bf16[4,128,1024]{1,2,0:T(8,128)(2,1)S(1)} %bitcast.134), kind=kOutput, calls=%fused_computation.62 | convolution fusion | flops 1074266112 | bytes 10485760 | tf_op jit(solution)/shard_map/gik,gjk->igj/dot_general | solution.py:42
  238.1 1.8 copy.85
  239.9 9.8 %all-to-all-start.2 = ((bf16[128,4,1024]{0,1,2:T(4,128)(2,1)}), bf16[128,4,1024]{0,1,2:T(4,128)(2,1)S(1)}, u32[]{:S(2)}, u32[]{:S(2)}) async-start(bf16[128,4,1024]{0,1,2:T(4,128)(2,1)} %copy.85), calls=%async_computation.2 | async-start | bytes 2097152 | tf_op jit(solution)/shard_map/all_to_all | solution.py:55
  249.9 28.7 %all-to-all-done.2 = bf16[128,4,1024]{0,1,2:T(4,128)(2,1)S(1)} async-done(((bf16[128,4,1024]{0,1,2:T(4,128)(2,1)}), bf16[128,4,1024]{0,1,2:T(4,128)(2,1)S(1)}, u32[]{:S(2)}, u32[]{:S(2)}) %all-to-all-start.2) | async-done | bytes 1048608 | tf_op jit(solution)/shard_map/all_to_all | solution.py:55
  278.6 0.1 copy.86
  278.7 0.2 fusion.36
  278.9 0.3 fusion.39
  279.3 0.4 fusion.41
  279.8 0.3 copy-done.3
  280.1 0.5 fusion.46
  280.6 1.2 convert_reduce_fusion
  281.8 0.3 fusion.4
  282.2 1.4 convolution_bitcast_fusion
  283.5 1.1 fusion.51
  284.7 1.7 copy.94
  286.3 5.0 all-to-all-start.3
  291.3 1.7 copy.96
  293.0 27.2 %all-to-all-done.3 = bf16[128,128,32]{1,2,0:T(8,128)(2,1)S(1)} async-done(((bf16[128,128,32]{1,2,0:T(8,128)(2,1)}), bf16[128,128,32]{1,2,0:T(8,128)(2,1)S(1)}, u32[]{:S(2)}, u32[]{:S(2)}) %all-to-all-start.3) | async-done | bytes 1048608 | tf_op jit(solution)/shard_map/all_to_all | solution.py:39
  320.2 5.0 all-to-all-start.4
  325.4 28.8 %all-to-all-done.4 = bf16[128,128,32]{1,2,0:T(8,128)(2,1)} async-done(((bf16[128,128,32]{1,2,0:T(8,128)(2,1)}), bf16[128,128,32]{1,2,0:T(8,128)(2,1)}, u32[]{:S(2)}, u32[]{:S(2)}) %all-to-all-start.4) | async-done | bytes 1048608 | tf_op jit(solution)/shard_map/all_to_all | solution.py:38
  354.3 1.3 copy.97
  355.6 5.6 %convert_bitcast_fusion = bf16[1024,4,1024]{0,2,1:T(8,128)(2,1)} fusion(bf16[4,128,1024]{1,2,0:T(8,128)(2,1)S(1)} %bitcast.125, bf16[4,128,1024]{1,2,0:T(8,128)(2,1)S(1)} %bitcast.126), kind=kOutput, calls=%fused_computation | convolution fusion | flops 1077936128 | bytes 10485760 | tf_op jit(solution)/shard_map/gki,gkj->igj/dot_general | solution.py:50
  361.2 79.6 %reduce-scatter.5.cloned.1.call-done = bf16[256,4,1024]{0,2,1:T(8,128)(2,1)} async-done(((bf16[1024,4,1024]{0,2,1:T(8,128)(2,1)}), bf16[256,4,1024]{0,2,1:T(8,128)(2,1)}) %reduce-scatter.5.cloned.1.call-update) | async-done | bytes 2097168 | tf_op jit(solution)/shard_map/reduce_scatter | solution.py:14
  440.8 4.1 copy.120
  445.0 36.6 %reduce-scatter.7.cloned.1.call-done = bf16[128,4096]{1,0:T(8,128)(2,1)} async-done(((bf16[256,4096]{1,0:T(8,128)(2,1)}), bf16[128,4096]{1,0:T(8,128)(2,1)}) %reduce-scatter.7.cloned.1.call-update) | async-done | bytes 1048592
  481.6 1.6 copy.121
  483.2 1.8 copy.99
  485.0 10.1 %all-to-all-start.5 = ((bf16[128,4,1024]{0,1,2:T(4,128)(2,1)}), bf16[128,4,1024]{0,1,2:T(4,128)(2,1)S(1)}, u32[]{:S(2)}, u32[]{:S(2)}) async-start(bf16[128,4,1024]{0,1,2:T(4,128)(2,1)} %copy.99), calls=%async_computation.6 | async-start | bytes 2097152 | tf_op jit(solution)/shard_map/all_to_all | solution.py:55
  495.3 1.9 fusion.55
  497.2 26.8 %all-to-all-done.5 = bf16[128,4,1024]{0,1,2:T(4,128)(2,1)S(1)} async-done(((bf16[128,4,1024]{0,1,2:T(4,128)(2,1)}), bf16[128,4,1024]{0,1,2:T(4,128)(2,1)S(1)}, u32[]{:S(2)}, u32[]{:S(2)}) %all-to-all-start.5) | async-done | bytes 1048608 | tf_op jit(solution)/shard_map/all_to_all | solution.py:55
  524.0 0.1 copy.100
  524.2 0.2 fusion.29
  524.4 0.3 fusion.32
  524.7 0.4 fusion.34
  525.2 1.1 copy-done
  526.3 1.0 fusion.11
  527.3 1.7 copy.105
  (37 shorter events, 1.1 us)
Async XLA Ops:
  6.5 2.6 copy-start.5
  6.5 2.6 copy-start.1
  6.5 225.8 %all-gather.2.cloned.1.call-start = ((), (), s32[]{:S(2)}) async-start(), calls=%async_computation.8 | async-start | bytes 9437184 | tf_op jit(solution)/shard_map/all_gather | solution.py:45
  238.1 11.6 %copy-start.6 = (f32[2,128]{1,0:T(2,128)S(1)}, f32[2,128]{1,0:T(2,128)}, u32[]{:S(2)}) copy-start(f32[2,128]{1,0:T(2,128)} %param.11) | copy-start | bytes 3076
  239.9 38.7 %all-to-all-start.2 = ((bf16[128,4,1024]{0,1,2:T(4,128)(2,1)}), bf16[128,4,1024]{0,1,2:T(4,128)(2,1)S(1)}, u32[]{:S(2)}, u32[]{:S(2)}) async-start(bf16[128,4,1024]{0,1,2:T(4,128)(2,1)} %copy.85), calls=%async_computation.2 | async-start | bytes 2097152 | tf_op jit(solution)/shard_map/all_to_all | solution.py:55
  279.2 0.8 copy-start.3
  279.8 0.9 copy-start.2
  286.3 33.9 %all-to-all-start.3 = ((bf16[128,128,32]{1,2,0:T(8,128)(2,1)}), bf16[128,128,32]{1,2,0:T(8,128)(2,1)S(1)}, u32[]{:S(2)}, u32[]{:S(2)}) async-start(bf16[128,128,32]{1,2,0:T(8,128)(2,1)} %copy.94), calls=%async_computation.3 | async-start | bytes 2097152 | tf_op jit(solution)/shard_map/all_to_all | solution.py:39
  320.2 34.0 %all-to-all-start.4 = ((bf16[128,128,32]{1,2,0:T(8,128)(2,1)}), bf16[128,128,32]{1,2,0:T(8,128)(2,1)}, u32[]{:S(2)}, u32[]{:S(2)}) async-start(bf16[128,128,32]{1,2,0:T(8,128)(2,1)} %copy.96), calls=%async_computation.4 | async-start | bytes 2097152 | tf_op jit(solution)/shard_map/all_to_all | solution.py:38
  325.3 115.5 %reduce-scatter.5.cloned.1.call-start = ((), (), s32[]{:S(2)}) async-start(), calls=%async_computation.9 | async-start | bytes 10485760 | tf_op jit(solution)/shard_map/reduce_scatter | solution.py:14
  361.2 120.4 %reduce-scatter.7.cloned.1.call-start = ((), (), s32[]{:S(2)}) async-start(), calls=%async_computation.10 | async-start | bytes 3145728
  485.0 39.0 %all-to-all-start.5 = ((bf16[128,4,1024]{0,1,2:T(4,128)(2,1)}), bf16[128,4,1024]{0,1,2:T(4,128)(2,1)S(1)}, u32[]{:S(2)}, u32[]{:S(2)}) async-start(bf16[128,4,1024]{0,1,2:T(4,128)(2,1)} %copy.99), calls=%async_computation.6 | async-start | bytes 2097152 | tf_op jit(solution)/shard_map/all_to_all | solution.py:55
  524.7 1.6 copy-start
  524.7 1.6 copy-start.4
Sparse Core Ops, SparseCore 0:
  55.4 176.9 all-gather.1
  361.3 79.5 reduce-scatter.4
  445.1 36.4 reduce-scatter.6
where the time goes:
time: 536 us; the launch traced here: 535 us
  waiting for transfers between devices  370 us (69%)
  blocking collectives  74.2 us (14%)
  starting transfers between devices  30 us (6%)
  local copies, waits for them, and re-layouts  24.2 us (5%)
  matrix products  18.5 us (3%)
  between operations  13.4 us (2%)
    all_gather x1, waiting for transfers between devices, local(): lax.all_gather(right_rows, ROW, axis=1, tiled=True)  142 us
    reduce_scatter x1, waiting for transfers between devices, sum_by_axis(): subtotal = lax.psum_scatter(subtotal, axis, scatter_dimension=0, tiled=True)  79.6 us
    all_to_all x2, waiting for transfers between devices, local(): lax.all_to_all(triangle.astype(jnp.bfloat16), 'col', split_axis=2, concat...  55.5 us
    all_to_all x1, blocking collectives, local(): lax.all_to_all(right_hand, 'col', split_axis=0, concat_axis=2, tiled=True)  40.5 us
    unnamed x4, waiting for transfers between devices  36.6 us
    all_to_all x1, blocking collectives, local(): lax.all_to_all(left_hand, 'col', split_axis=0, concat_axis=2, tiled=True)  33.7 us
    all_to_all x1, waiting for transfers between devices, local(): lax.all_to_all(left_hand, 'col', split_axis=0, concat_axis=2, tiled=True)  28.8 us
    all_to_all x1, waiting for transfers between devices, local(): lax.all_to_all(right_hand, 'col', split_axis=0, concat_axis=2, tiled=True)  27.2 us
  transfers between devices with their start and end apart: 7, of which 7 were waited for; matrix products, arithmetic and copies ran while one was open for 1% of the time, Pallas kernels for 0%

commit v1 on v0

--- a/solution.py
+++ b/solution.py
@@ -42,7 +42,9 @@
             triangle = jnp.einsum(
                 "gik,gjk->igj",
                 left_rows,
-                lax.all_gather(right_rows, ROW, axis=1, tiled=True),
+                jnp.concatenate(
+                    lax.all_to_all(jnp.stack([right_rows] * lax.axis_size(ROW)), ROW, 0, 0), axis=1
+                ),
                 preferred_element_type=jnp.float32,
             )
         else:

time: 536 us -> 498 us (0.929)
  blocking collectives: 74.2 us -> 0 us
  starting transfers between devices: 30 us -> 47.4 us
  local copies, waits for them, and re-layouts: 24.2 us -> 38.6 us
    all_gather x1 -> x0, waiting for transfers between devices: 142 us -> none  [local(): lax.all_gather(right_rows, ROW, axis=1, tiled=True)]
    all_to_all x0 -> x1, waiting for transfers between devices: none -> 94.1 us  [local(): lax.all_to_all(jnp.stack([right_rows] * lax.axis_size(ROW)), ROW, 0, 0)]
    all_to_all x2 -> x0, blocking collectives: 74.2 us -> none  [the longest x1 40.5 us: local(): lax.all_to_all(right_hand, 'col', split_axis=0, concat_axis=2, tiled=True)]
    all_to_all x1 -> x2, waiting for transfers between devices: 27.2 us -> 54.4 us  [local(): lax.all_to_all(right_hand, 'col', split_axis=0, concat_axis=2, tiled=True)]
    all_to_all x1 -> x2, waiting for transfers between devices: 28.8 us -> 55.2 us  [local(): lax.all_to_all(left_hand, 'col', split_axis=0, concat_axis=2, tiled=True)]
    all_to_all x1 -> x2, starting transfers between devices: 4.99 us -> 16.6 us  [local(): lax.all_to_all(right_hand, 'col', split_axis=0, concat_axis=2, tiled=True)]
    reshape x0 -> x1, local copies, waits for them, and re-layouts: none -> 8.18 us  [local(): jnp.concatenate(lax.all_to_all(jnp.stack([right_rows] * lax.axis_size(ROW...]
    another operation x0 -> x2, local copies, waits for them, and re-layouts: none -> 5.78 us  [local(): jnp.stack([right_rows] * lax.axis_size(ROW))]
  transfers between devices with their start and end apart: 7 -> 9, of which waited for: 7 -> 9; matrix products, arithmetic and copies ran while one was open for 1% -> 2% of each run, Pallas kernels for 0% -> 0%
where the time goes in v1:
time: 498 us; the launch traced here: 497 us
  waiting for transfers between devices  374 us (75%)
  starting transfers between devices  47.4 us (10%)
  local copies, waits for them, and re-layouts  38.6 us (8%)
  matrix products  18.5 us (4%)
  between operations  13.7 us (3%)
  other arithmetic  4.98 us (1%)
    all_to_all x1, waiting for transfers between devices, local(): lax.all_to_all(jnp.stack([right_rows] * lax.axis_size(ROW)), ROW, 0, 0)  94.1 us
    reduce_scatter x1, waiting for transfers between devices, sum_by_axis(): subtotal = lax.psum_scatter(subtotal, axis, scatter_dimension=0, tiled=True)  77.8 us
    all_to_all x2, waiting for transfers between devices, local(): lax.all_to_all(triangle.astype(jnp.bfloat16), 'col', split_axis=2, concat...  55.5 us
    all_to_all x2, waiting for transfers between devices, local(): lax.all_to_all(left_hand, 'col', split_axis=0, concat_axis=2, tiled=True)  55.2 us
    all_to_all x2, waiting for transfers between devices, local(): lax.all_to_all(right_hand, 'col', split_axis=0, concat_axis=2, tiled=True)  54.4 us
    unnamed x3, waiting for transfers between devices  36.6 us
    all_to_all x2, starting transfers between devices, local(): lax.all_to_all(right_hand, 'col', split_axis=0, concat_axis=2, tiled=True)  16.6 us
    all_to_all x2, starting transfers between devices, local(): lax.all_to_all(triangle.astype(jnp.bfloat16), 'col', split_axis=2, concat...  15.6 us
  transfers between devices with their start and end apart: 9, of which 9 were waited for; matrix products, arithmetic and copies ran while one was open for 2% of the time, Pallas kernels for 0%

profile of v1, /device:TPU:4, one launch (start us, length us, event | category | flops | bytes accessed | tf_op | source)
XLA Modules:
  0.0 496.8 jit_solution(4690677529215169085)
XLA Ops:
  6.5 2.0 copy.75
  8.7 0.3 fusion.7
  9.1 1.4 convolution_bitcast_fusion.1
  10.5 1.1 fusion.49
  11.6 1.7 copy.79
  13.3 11.6 %all-to-all-start = ((bf16[128,128,32]{1,2,0:T(8,128)(2,1)}), bf16[128,128,32]{1,2,0:T(8,128)(2,1)S(1)}, u32[]{:S(2)}, u32[]{:S(2)}) async-start(bf16[128,128,32]{1,2,0:T(8,128)(2,1)} %copy.79), calls=%async_computation | async-start | bytes 2097152 | tf_op jit(solution)/shard_map/all_to_all | solution.py:39
  24.9 1.7 copy.83
  26.6 27.2 %all-to-all-done = bf16[128,128,32]{1,2,0:T(8,128)(2,1)S(1)} async-done(((bf16[128,128,32]{1,2,0:T(8,128)(2,1)}), bf16[128,128,32]{1,2,0:T(8,128)(2,1)S(1)}, u32[]{:S(2)}, u32[]{:S(2)}) %all-to-all-start) | async-done | bytes 1048608 | tf_op jit(solution)/shard_map/all_to_all | solution.py:39
  53.8 5.0 %all-to-all-start.2 = ((bf16[128,128,32]{1,2,0:T(8,128)(2,1)}), bf16[128,128,32]{1,2,0:T(8,128)(2,1)S(1)}, u32[]{:S(2)}, u32[]{:S(2)}) async-start(bf16[128,128,32]{1,2,0:T(8,128)(2,1)} %copy.83), calls=%async_computation.2 | async-start | bytes 2097152 | tf_op jit(solution)/shard_map/all_to_all | solution.py:38
  58.8 1.1 copy.80
  59.9 1.5 copy.81
  61.4 26.4 %all-to-all-done.2 = bf16[128,128,32]{1,2,0:T(8,128)(2,1)S(1)} async-done(((bf16[128,128,32]{1,2,0:T(8,128)(2,1)}), bf16[128,128,32]{1,2,0:T(8,128)(2,1)S(1)}, u32[]{:S(2)}, u32[]{:S(2)}) %all-to-all-start.2) | async-done | bytes 1048608 | tf_op jit(solution)/shard_map/all_to_all | solution.py:38
  87.7 4.3 stack.5
  92.0 5.1 %all-to-all-start.1 = ((bf16[8,4,128,1024]{3,2,1,0:T(8,128)(2,1)}), bf16[8,4,128,1024]{3,2,1,0:T(8,128)(2,1)}, u32[]{:S(2)}, u32[]{:S(2)}) async-start(bf16[8,4,128,1024]{3,2,1,0:T(8,128)(2,1)} %stack.5), calls=%async_computation.1 | async-start | bytes 16777216 | tf_op jit(solution)/shard_map/all_to_all | solution.py:46
  97.2 94.1 %all-to-all-done.1 = bf16[8,4,128,1024]{3,2,1,0:T(8,128)(2,1)} async-done(((bf16[8,4,128,1024]{3,2,1,0:T(8,128)(2,1)}), bf16[8,4,128,1024]{3,2,1,0:T(8,128)(2,1)}, u32[]{:S(2)}, u32[]{:S(2)}) %all-to-all-start.1) | async-done | bytes 8388640 | tf_op jit(solution)/shard_map/all_to_all | solution.py:46
  191.3 8.2 %copy.82 = bf16[4,8,128,1024]{3,2,1,0:T(8,128)(2,1)} copy(bf16[4,8,128,1024]{3,2,0,1:T(8,128)(2,1)} %bitcast.11) | data formatting | bytes 16777216 | tf_op jit(solution)/shard_map/reshape | solution.py:45
  199.5 5.7 %fusion.42 = bf16[128,4,1024]{0,2,1:T(8,128)(2,1)S(1)} fusion(bf16[4,1024,1024]{2,1,0:T(8,128)(2,1)} %bitcast.127, bf16[4,128,1024]{1,2,0:T(8,128)(2,1)S(1)} %bitcast.137), kind=kOutput, calls=%fused_computation.62 | convolution fusion | flops 1074266112 | bytes 10485760 | tf_op jit(solution)/shard_map/gik,gjk->igj/dot_general | solution.py:42
  205.2 1.8 copy.86
  207.0 5.5 %all-to-all-start.3 = ((bf16[128,4,1024]{0,1,2:T(4,128)(2,1)}), bf16[128,4,1024]{0,1,2:T(4,128)(2,1)S(1)}, u32[]{:S(2)}, u32[]{:S(2)}) async-start(bf16[128,4,1024]{0,1,2:T(4,128)(2,1)} %copy.86), calls=%async_computation.3 | async-start | bytes 2097152 | tf_op jit(solution)/shard_map/all_to_all | solution.py:57
  212.7 28.7 %all-to-all-done.3 = bf16[128,4,1024]{0,1,2:T(4,128)(2,1)S(1)} async-done(((bf16[128,4,1024]{0,1,2:T(4,128)(2,1)}), bf16[128,4,1024]{0,1,2:T(4,128)(2,1)S(1)}, u32[]{:S(2)}, u32[]{:S(2)}) %all-to-all-start.3) | async-done | bytes 1048608 | tf_op jit(solution)/shard_map/all_to_all | solution.py:57
  241.7 0.3 fusion.39
  242.1 0.4 fusion.41
  242.9 0.5 fusion.46
  243.4 1.2 convert_reduce_fusion
  244.6 0.3 fusion.4
  244.9 1.4 convolution_bitcast_fusion
  246.3 1.1 fusion.51
  247.4 1.7 copy.95
  249.1 5.0 %all-to-all-start.4 = ((bf16[128,128,32]{1,2,0:T(8,128)(2,1)}), bf16[128,128,32]{1,2,0:T(8,128)(2,1)S(1)}, u32[]{:S(2)}, u32[]{:S(2)}) async-start(bf16[128,128,32]{1,2,0:T(8,128)(2,1)} %copy.95), calls=%async_computation.4 | async-start | bytes 2097152 | tf_op jit(solution)/shard_map/all_to_all | solution.py:39
  254.1 1.7 copy.97
  255.8 27.2 %all-to-all-done.4 = bf16[128,128,32]{1,2,0:T(8,128)(2,1)S(1)} async-done(((bf16[128,128,32]{1,2,0:T(8,128)(2,1)}), bf16[128,128,32]{1,2,0:T(8,128)(2,1)S(1)}, u32[]{:S(2)}, u32[]{:S(2)}) %all-to-all-start.4) | async-done | bytes 1048608 | tf_op jit(solution)/shard_map/all_to_all | solution.py:39
  283.0 5.0 %all-to-all-start.5 = ((bf16[128,128,32]{1,2,0:T(8,128)(2,1)}), bf16[128,128,32]{1,2,0:T(8,128)(2,1)}, u32[]{:S(2)}, u32[]{:S(2)}) async-start(bf16[128,128,32]{1,2,0:T(8,128)(2,1)} %copy.97), calls=%async_computation.5 | async-start | bytes 2097152 | tf_op jit(solution)/shard_map/all_to_all | solution.py:38
  288.2 28.8 %all-to-all-done.5 = bf16[128,128,32]{1,2,0:T(8,128)(2,1)} async-done(((bf16[128,128,32]{1,2,0:T(8,128)(2,1)}), bf16[128,128,32]{1,2,0:T(8,128)(2,1)}, u32[]{:S(2)}, u32[]{:S(2)}) %all-to-all-start.5) | async-done | bytes 1048608 | tf_op jit(solution)/shard_map/all_to_all | solution.py:38
  317.1 1.3 copy.98
  318.4 5.6 %convert_bitcast_fusion = bf16[1024,4,1024]{0,2,1:T(8,128)(2,1)} fusion(bf16[4,128,1024]{1,2,0:T(8,128)(2,1)S(1)} %bitcast.128, bf16[4,128,1024]{1,2,0:T(8,128)(2,1)S(1)} %bitcast.129), kind=kOutput, calls=%fused_computation | convolution fusion | flops 1077936128 | bytes 10485760 | tf_op jit(solution)/shard_map/gki,gkj->igj/dot_general | solution.py:52
  324.0 77.8 %reduce-scatter.5.cloned.1.call-done = bf16[256,4,1024]{0,2,1:T(8,128)(2,1)} async-done(((bf16[1024,4,1024]{0,2,1:T(8,128)(2,1)}), bf16[256,4,1024]{0,2,1:T(8,128)(2,1)}) %reduce-scatter.5.cloned.1.call-update) | async-done | bytes 2097168 | tf_op jit(solution)/shard_map/reduce_scatter | solution.py:14
  401.9 4.1 copy.121
  406.0 36.6 %reduce-scatter.7.cloned.1.call-done = bf16[128,4096]{1,0:T(8,128)(2,1)} async-done(((bf16[256,4096]{1,0:T(8,128)(2,1)}), bf16[128,4096]{1,0:T(8,128)(2,1)}) %reduce-scatter.7.cloned.1.call-update) | async-done | bytes 1048592
  442.6 1.6 copy.122
  444.2 1.8 copy.100
  446.0 10.1 %all-to-all-start.6 = ((bf16[128,4,1024]{0,1,2:T(4,128)(2,1)}), bf16[128,4,1024]{0,1,2:T(4,128)(2,1)S(1)}, u32[]{:S(2)}, u32[]{:S(2)}) async-start(bf16[128,4,1024]{0,1,2:T(4,128)(2,1)} %copy.100), calls=%async_computation.7 | async-start | bytes 2097152 | tf_op jit(solution)/shard_map/all_to_all | solution.py:57
  456.3 1.9 fusion.55
  458.2 26.8 %all-to-all-done.6 = bf16[128,4,1024]{0,1,2:T(4,128)(2,1)S(1)} async-done(((bf16[128,4,1024]{0,1,2:T(4,128)(2,1)}), bf16[128,4,1024]{0,1,2:T(4,128)(2,1)S(1)}, u32[]{:S(2)}, u32[]{:S(2)}) %all-to-all-start.6) | async-done | bytes 1048608 | tf_op jit(solution)/shard_map/all_to_all | solution.py:57
  485.4 0.3 fusion.32
  485.7 0.4 fusion.34
  486.2 1.1 copy-done
  487.3 1.0 fusion.11
  488.3 1.7 copy.106
  (40 shorter events, 2.2 us)
Async XLA Ops:
  6.5 2.6 copy-start.5
  6.5 2.6 copy-start.1
  13.3 40.5 %all-to-all-start = ((bf16[128,128,32]{1,2,0:T(8,128)(2,1)}), bf16[128,128,32]{1,2,0:T(8,128)(2,1)S(1)}, u32[]{:S(2)}, u32[]{:S(2)}) async-start(bf16[128,128,32]{1,2,0:T(8,128)(2,1)} %copy.79), calls=%async_computation | async-start | bytes 2097152 | tf_op jit(solution)/shard_map/all_to_all | solution.py:39
  53.8 33.9 %all-to-all-start.2 = ((bf16[128,128,32]{1,2,0:T(8,128)(2,1)}), bf16[128,128,32]{1,2,0:T(8,128)(2,1)S(1)}, u32[]{:S(2)}, u32[]{:S(2)}) async-start(bf16[128,128,32]{1,2,0:T(8,128)(2,1)} %copy.83), calls=%async_computation.2 | async-start | bytes 2097152 | tf_op jit(solution)/shard_map/all_to_all | solution.py:38
  92.0 99.3 %all-to-all-start.1 = ((bf16[8,4,128,1024]{3,2,1,0:T(8,128)(2,1)}), bf16[8,4,128,1024]{3,2,1,0:T(8,128)(2,1)}, u32[]{:S(2)}, u32[]{:S(2)}) async-start(bf16[8,4,128,1024]{3,2,1,0:T(8,128)(2,1)} %stack.5), calls=%async_computation.1 | async-start | bytes 16777216 | tf_op jit(solution)/shard_map/all_to_all | solution.py:46
  205.2 7.3 %copy-start.6 = (f32[2,128]{1,0:T(2,128)S(1)}, f32[2,128]{1,0:T(2,128)}, u32[]{:S(2)}) copy-start(f32[2,128]{1,0:T(2,128)} %param.11) | copy-start | bytes 3076
  207.0 34.4 %all-to-all-start.3 = ((bf16[128,4,1024]{0,1,2:T(4,128)(2,1)}), bf16[128,4,1024]{0,1,2:T(4,128)(2,1)S(1)}, u32[]{:S(2)}, u32[]{:S(2)}) async-start(bf16[128,4,1024]{0,1,2:T(4,128)(2,1)} %copy.86), calls=%async_computation.3 | async-start | bytes 2097152 | tf_op jit(solution)/shard_map/all_to_all | solution.py:57
  242.0 0.8 copy-start.3
  242.5 0.9 copy-start.2
  249.1 33.9 %all-to-all-start.4 = ((bf16[128,128,32]{1,2,0:T(8,128)(2,1)}), bf16[128,128,32]{1,2,0:T(8,128)(2,1)S(1)}, u32[]{:S(2)}, u32[]{:S(2)}) async-start(bf16[128,128,32]{1,2,0:T(8,128)(2,1)} %copy.95), calls=%async_computation.4 | async-start | bytes 2097152 | tf_op jit(solution)/shard_map/all_to_all | solution.py:39
  283.0 34.0 %all-to-all-start.5 = ((bf16[128,128,32]{1,2,0:T(8,128)(2,1)}), bf16[128,128,32]{1,2,0:T(8,128)(2,1)}, u32[]{:S(2)}, u32[]{:S(2)}) async-start(bf16[128,128,32]{1,2,0:T(8,128)(2,1)} %copy.97), calls=%async_computation.5 | async-start | bytes 2097152 | tf_op jit(solution)/shard_map/all_to_all | solution.py:38
  288.1 113.8 %reduce-scatter.5.cloned.1.call-start = ((), (), s32[]{:S(2)}) async-start(), calls=%async_computation.9 | async-start | bytes 10485760 | tf_op jit(solution)/shard_map/reduce_scatter | solution.py:14
  324.0 118.6 %reduce-scatter.7.cloned.1.call-start = ((), (), s32[]{:S(2)}) async-start(), calls=%async_computation.10 | async-start | bytes 3145728
  446.0 39.0 %all-to-all-start.6 = ((bf16[128,4,1024]{0,1,2:T(4,128)(2,1)}), bf16[128,4,1024]{0,1,2:T(4,128)(2,1)S(1)}, u32[]{:S(2)}, u32[]{:S(2)}) async-start(bf16[128,4,1024]{0,1,2:T(4,128)(2,1)} %copy.100), calls=%async_computation.7 | async-start | bytes 2097152 | tf_op jit(solution)/shard_map/all_to_all | solution.py:57
  485.7 1.6 copy-start
  485.7 1.6 copy-start.4
Sparse Core Ops, SparseCore 0:
  324.1 77.7 reduce-scatter.4
  406.1 36.4 reduce-scatter.6
